TPU v7x, 32 devices: a whole 2x2x4 slice. The times are simulated.
32 devices in a mesh: win: 8 (over z, y), tile: 4 (over x, core).
Axes of the slice: x: 2, y: 2, z: 4, core: 2. Of those that a mesh axis runs over, the one named last changes fastest.
Arguments:
- right_side: float32 [8, 2, 128, 1024], P('win', None, 'tile'), may hold values from -64 to 64
- error_weight: float32 [8, 2, 128, 1024], P('win', None, 'tile'), may hold values from 0.5 to 4
- coeffs: float32 [4, 8, 2, 128, 1024], P(None, 'win', None, 'tile'), may hold values from 0.1 to 0.4
- obs_block: int32 [8, 128], P('win', 'tile'), may hold values from 0 to 511
- obs_pos: int32 [8, 128, 128], P('win', 'tile'), may hold values from 0 to 127
- obs_weight: float32 [8, 128, 128], P('win', 'tile'), may hold values from 0.5 to 4
Outputs:
- solution_field: float32 [8, 2, 128, 1024], P('win', None, 'tile')
- residual: float32 [8, 2, 128, 1024], P('win', None, 'tile')
All inputs are finite; a program needn't handle non-finite values.
Results may differ from a plain program's by a relative error of at most 0.0001.
Values sent between devices are 32-bit elements; how exact they have to be, the bound alone decides.
A program may use at most 64 MiB of HBM per device.

v0:
```python
import jax
import jax.numpy as jnp
from jax import lax
from jax.sharding import PartitionSpec as P

ITERS = 3


def extended(block, sides, width):
    for axis, dim in sides:
        count = lax.axis_size(axis)
        forward = [(i, i + 1) for i in range(count - 1)]
        backward = [(target, source) for source, target in forward]
        low = lax.ppermute(
            lax.slice_in_dim(block, block.shape[dim] - width, None, axis=dim), axis, forward
        )
        high = lax.ppermute(lax.slice_in_dim(block, 0, width, axis=dim), axis, backward)
        block = jnp.concatenate([low, block, high], axis=dim)
    return block


def passed_along(x, axis, by):
    devices = lax.axis_size(axis)
    pairs = [(i, i + by) for i in range(devices) if 0 <= i + by < devices]
    return lax.ppermute(x, axis, pairs)


def forward(state, coeffs):
    padded = extended(state, (("tile", 2),), 1)
    north_south = padded[:, :, 2:, :] + padded[:, :, :-2, :]
    return (
        coeffs[0] * state
        + coeffs[1] * north_south
        + coeffs[2] * jnp.roll(state, -1, axis=3)
        + coeffs[3] * jnp.roll(state, 1, axis=3)
    )


def backward(state, coeffs):
    spread = extended(coeffs[1] * state, (("tile", 2),), 1)
    north_south = spread[:, :, 2:, :] + spread[:, :, :-2, :]
    return (
        coeffs[0] * state
        + north_south
        + jnp.roll(coeffs[2] * state, 1, axis=3)
        + jnp.roll(coeffs[3] * state, -1, axis=3)
    )


def observe(state, block_hot, cell_hot, obs_weight):
    width = cell_hot.shape[2]
    block_rows = state.reshape(-1, width)
    picked = jnp.dot(
        block_hot, block_rows, precision=lax.Precision.HIGHEST, preferred_element_type=jnp.float32
    )
    observed = jnp.einsum("bjc,bc->bj", cell_hot, picked, precision=lax.Precision.HIGHEST)
    weighted = observed * obs_weight[0]
    returned = jnp.einsum("bjc,bj->bc", cell_hot, weighted, precision=lax.Precision.HIGHEST)
    spread = jnp.dot(
        block_hot.T, returned, precision=lax.Precision.HIGHEST, preferred_element_type=jnp.float32
    )
    return spread.reshape(state.shape)


def on_device(right_side, error_weight, coeffs, obs_block, obs_pos, obs_weight):
    width = obs_pos.shape[2]
    block_total = right_side.size // width
    block_hot = (obs_block[0][:, None] == jnp.arange(block_total, dtype=jnp.int32)[None, :]).astype(
        jnp.float32
    )
    cell_hot = (obs_pos[0][:, :, None] == jnp.arange(width, dtype=jnp.int32)[None, None, :]).astype(
        jnp.float32
    )

    def hessian(state):
        propagated = forward(state, coeffs)
        before = passed_along(propagated, "win", 1)
        weighted = error_weight * (state - before)
        following = passed_along(weighted, "win", -1)
        return (
            weighted - backward(following, coeffs) + observe(state, block_hot, cell_hot, obs_weight)
        )

    def two_products(vector, image_vec):
        return lax.psum((jnp.sum(vector * vector), jnp.sum(vector * image_vec)), ("win", "tile"))

    solution_field = jnp.zeros_like(right_side)
    residual = right_side
    product_vec = hessian(residual)
    norm_now, product = two_products(residual, product_vec)
    step_length = norm_now / product
    direction = residual
    along = product_vec
    for iteration in range(ITERS):
        solution_field = solution_field + step_length * direction
        residual = residual - step_length * along
        if iteration + 1 < ITERS:
            product_vec = hessian(residual)
            norm_next, product = two_products(residual, product_vec)
            beta_ratio = norm_next / norm_now
            step_length = norm_next / (product - beta_ratio * norm_next / step_length)
            direction = residual + beta_ratio * direction
            along = product_vec + beta_ratio * along
            norm_now = norm_next
    return (solution_field, residual)


def solution(mesh):
    in_specs = (
        P("win", None, "tile", None),
        P("win", None, "tile", None),
        P(None, "win", None, "tile", None),
        P("win", "tile"),
        P("win", "tile", None),
        P("win", "tile", None),
    )
    out_specs = (P("win", None, "tile", None), P("win", None, "tile", None))
    return jax.shard_map(
        on_device, mesh=mesh, in_specs=in_specs, out_specs=out_specs, check_vma=False
    )
```

profile of v0, /device:TPU:0, one launch (start us, length us, event | category | flops | bytes accessed | tf_op | source)
XLA Modules:
  0.0 242.9 jit_solution(11518069762869927047)
XLA Ops:
  0.7 1.0 fusion.71
  1.6 2.4 collective-permute-start.1
  4.0 1.3 collective-permute-start
  5.3 1.2 fusion.70
  6.5 0.1 fusion.69
  6.7 2.5 %collective-permute-done = f32[1,2,1,1024]{3,2,1,0:T(1,128)S(1)} collective-permute-done((f32[1,2,1,1024]{3,2,1,0:T(1,128)S(1)}, f32[1,2,1,1024]{3,2,1,0:T(1,128)S(1)}, u32[]{:S(2)}, u32[]{:S(2)}) %collective-permute-start) | collective-permute-done | bytes 8224 | tf_op jit(solution)/shard_map/ppermute | solution.py:17
  9.2 0.2 fusion.44
  9.4 3.6 %collective-permute-start.2 = (f32[1,2,32,1024]{3,2,1,0:T(8,128)S(1)}, f32[1,2,32,1024]{3,2,1,0:T(8,128)S(1)}, u32[]{:S(2)}, u32[]{:S(2)}) collective-permute-start(f32[1,2,32,1024]{3,2,1,0:T(8,128)S(1)} %fusion.44), channel_id=1, source_target_pairs={{0,4},{4,8},{8,12},{12,16},{16,20},{20,24},{24,28},{1,5},{5,9},{9,... | collective-permute-start | bytes 786440 | tf_op jit(solution)/shard_map/ppermute | solution.py:25
  13.0 0.2 fusion.50
  13.3 2.0 fusion.5
  15.3 3.0 %collective-permute-done.2 = f32[1,2,32,1024]{3,2,1,0:T(8,128)S(1)} collective-permute-done((f32[1,2,32,1024]{3,2,1,0:T(8,128)S(1)}, f32[1,2,32,1024]{3,2,1,0:T(8,128)S(1)}, u32[]{:S(2)}, u32[]{:S(2)}) %collective-permute-start.2) | collective-permute-done | bytes 262176 | tf_op jit(solution)/shard_map/ppermute | solution.py:25
  18.3 1.3 collective-permute-start.3
  19.6 1.5 fusion.4
  21.1 8.2 %collective-permute-done.3 = f32[1,2,32,1024]{3,2,1,0:T(8,128)S(1)} collective-permute-done((f32[1,2,32,1024]{3,2,1,0:T(8,128)S(1)}, f32[1,2,32,1024]{3,2,1,0:T(8,128)S(1)}, u32[]{:S(2)}, u32[]{:S(2)}) %collective-permute-start.3) | collective-permute-done | bytes 262176 | tf_op jit(solution)/shard_map/ppermute | solution.py:25
  29.4 2.3 collective-permute-start.5
  31.6 1.3 collective-permute-start.4
  32.9 0.5 fusion.49
  33.5 0.1 slice.248
  33.6 0.1 slice.246
  33.7 1.0 collective-permute-done.4
  34.7 0.8 multiply_reduce_fusion.4
  35.5 42.5 %all-reduce.2 = (f32[]{:T(128)}, f32[]{:T(128)}) all-reduce(f32[]{:T(128)} %get-tuple-element.7, f32[]{:T(128)} %get-tuple-element.6), channel_id=1, replica_groups=mesh['win'=8,'tile'=4] {'win','tile'}, use_global_device_ids=true, to_apply=%region_1.2 | all-reduce | flops 2 | bytes 16 | tf_op jit(solution)/shard_map/psum | solution.py:85
  79.4 0.1 fusion.66
  79.5 1.3 collective-permute-start.7
  80.8 1.3 collective-permute-start.6
  82.1 0.1 fusion.65
  82.3 4.1 %collective-permute-done.6 = f32[1,2,1,1024]{3,2,1,0:T(1,128)S(1)} collective-permute-done((f32[1,2,1,1024]{3,2,1,0:T(1,128)S(1)}, f32[1,2,1,1024]{3,2,1,0:T(1,128)S(1)}, u32[]{:S(2)}, u32[]{:S(2)}) %collective-permute-start.6) | collective-permute-done | bytes 8224 | tf_op jit(solution)/shard_map/ppermute | solution.py:17
  86.4 0.2 fusion.33
  86.6 2.7 %collective-permute-start.8 = (f32[1,2,32,1024]{3,2,1,0:T(8,128)S(1)}, f32[1,2,32,1024]{3,2,1,0:T(8,128)S(1)}, u32[]{:S(2)}, u32[]{:S(2)}) collective-permute-start(f32[1,2,32,1024]{3,2,1,0:T(8,128)S(1)} %fusion.33), channel_id=1, source_target_pairs={{0,4},{4,8},{8,12},{12,16},{16,20},{20,24},{24,28},{1,5},{5,9},{9,... | collective-permute-start | bytes 786440 | tf_op jit(solution)/shard_map/ppermute | solution.py:25
  89.3 0.2 fusion.48
  89.5 2.0 fusion.3
  91.5 3.0 %collective-permute-done.8 = f32[1,2,32,1024]{3,2,1,0:T(8,128)S(1)} collective-permute-done((f32[1,2,32,1024]{3,2,1,0:T(8,128)S(1)}, f32[1,2,32,1024]{3,2,1,0:T(8,128)S(1)}, u32[]{:S(2)}, u32[]{:S(2)}) %collective-permute-start.8) | collective-permute-done | bytes 262176 | tf_op jit(solution)/shard_map/ppermute | solution.py:25
  94.6 1.3 collective-permute-start.9
  95.9 1.5 fusion.2
  97.4 8.2 %collective-permute-done.9 = f32[1,2,32,1024]{3,2,1,0:T(8,128)S(1)} collective-permute-done((f32[1,2,32,1024]{3,2,1,0:T(8,128)S(1)}, f32[1,2,32,1024]{3,2,1,0:T(8,128)S(1)}, u32[]{:S(2)}, u32[]{:S(2)}) %collective-permute-start.9) | collective-permute-done | bytes 262176 | tf_op jit(solution)/shard_map/ppermute | solution.py:25
  105.7 2.3 collective-permute-start.11
  108.0 1.3 collective-permute-start.10
  109.3 1.2 fusion.47
  110.4 1.0 reshape.243
  111.5 0.1 slice.260
  111.6 0.1 slice.258
  111.7 1.8 multiply_reduce_fusion.2
  113.5 42.6 %all-reduce.1 = (f32[]{:T(128)}, f32[]{:T(128)}) all-reduce(f32[]{:T(128)} %get-tuple-element.5, f32[]{:T(128)} %get-tuple-element.4), channel_id=1, replica_groups=mesh['win'=8,'tile'=4] {'win','tile'}, use_global_device_ids=true, to_apply=%region_5.6 | all-reduce | flops 2 | bytes 16 | tf_op jit(solution)/shard_map/psum | solution.py:85
  160.9 0.1 fusion.62
  161.0 1.3 collective-permute-start.13
  162.3 1.3 collective-permute-start.12
  163.6 0.1 fusion.61
  163.7 4.1 %collective-permute-done.12 = f32[1,2,1,1024]{3,2,1,0:T(1,128)S(1)} collective-permute-done((f32[1,2,1,1024]{3,2,1,0:T(1,128)S(1)}, f32[1,2,1,1024]{3,2,1,0:T(1,128)S(1)}, u32[]{:S(2)}, u32[]{:S(2)}) %collective-permute-start.12) | collective-permute-done | bytes 8224 | tf_op jit(solution)/shard_map/ppermute | solution.py:17
  167.9 0.2 fusion.22
  168.1 2.4 collective-permute-start.14
  170.4 0.2 fusion.46
  170.7 2.0 fusion.1
  172.7 3.0 %collective-permute-done.14 = f32[1,2,32,1024]{3,2,1,0:T(8,128)S(1)} collective-permute-done((f32[1,2,32,1024]{3,2,1,0:T(8,128)S(1)}, f32[1,2,32,1024]{3,2,1,0:T(8,128)S(1)}, u32[]{:S(2)}, u32[]{:S(2)}) %collective-permute-start.14) | collective-permute-done | bytes 262176 | tf_op jit(solution)/shard_map/ppermute | solution.py:25
  175.7 1.3 collective-permute-start.15
  177.0 1.5 fusion
  178.5 8.2 %collective-permute-done.15 = f32[1,2,32,1024]{3,2,1,0:T(8,128)S(1)} collective-permute-done((f32[1,2,32,1024]{3,2,1,0:T(8,128)S(1)}, f32[1,2,32,1024]{3,2,1,0:T(8,128)S(1)}, u32[]{:S(2)}, u32[]{:S(2)}) %collective-permute-start.15) | collective-permute-done | bytes 262176 | tf_op jit(solution)/shard_map/ppermute | solution.py:25
  186.8 2.3 collective-permute-start.17
  189.1 1.3 collective-permute-start.16
  190.4 1.2 fusion.45
  191.6 1.7 reshape.245
  193.3 0.1 slice.272
  193.5 1.8 multiply_reduce_fusion
  195.3 42.6 %all-reduce = (f32[]{:T(128)}, f32[]{:T(128)}) all-reduce(f32[]{:T(128)} %get-tuple-element.3, f32[]{:T(128)} %get-tuple-element.2), channel_id=1, replica_groups=mesh['win'=8,'tile'=4] {'win','tile'}, use_global_device_ids=true, to_apply=%region_9.10 | all-reduce | flops 2 | bytes 16 | tf_op jit(solution)/shard_map/psum | solution.py:85
  241.9 0.9 multiply_subtract_fusion
  (48 shorter events, 0.8 us)
Async XLA Ops:
  0.6 5.9 %copy-start.1 = (f32[1,2,32,1024]{3,2,1,0:T(8,128)S(1)}, f32[1,2,32,1024]{3,2,1,0:T(8,128)}, u32[]{:S(2)}) copy-start(f32[1,2,32,1024]{3,2,1,0:T(8,128)} %param.6) | copy-start | bytes 786436
  0.6 8.6 %copy-start = (f32[4,1,2,32,1024]{4,3,2,1,0:T(8,128)S(1)}, f32[4,1,2,32,1024]{4,3,2,1,0:T(8,128)}, u32[]{:S(2)}) copy-start(f32[4,1,2,32,1024]{4,3,2,1,0:T(8,128)} %param.8) | copy-start | bytes 3145732
  1.6 5.0 %collective-permute-start.1 = (f32[1,2,1,1024]{3,2,1,0:T(1,128)S(1)}, f32[1,2,1,1024]{3,2,1,0:T(1,128)S(1)}, u32[]{:S(2)}, u32[]{:S(2)}) collective-permute-start(f32[1,2,1,1024]{3,2,1,0:T(1,128)S(1)} %get-tuple-element.51), channel_id=1, source_target_pairs={{0,1},{1,2},{2,3},{4,5},{5,6},{6,7},{8,9},{9,10},{10,11},{12,13},{... | collective-permute-start | bytes 24584 | tf_op jit(solution)/shard_map/ppermute | solution.py:14
  4.0 5.2 %collective-permute-start = (f32[1,2,1,1024]{3,2,1,0:T(1,128)S(1)}, f32[1,2,1,1024]{3,2,1,0:T(1,128)S(1)}, u32[]{:S(2)}, u32[]{:S(2)}) collective-permute-start(f32[1,2,1,1024]{3,2,1,0:T(1,128)S(1)} %get-tuple-element.50), channel_id=1, source_target_pairs={{1,0},{2,1},{3,2},{5,4},{6,5},{7,6},{9,8},{10,9},{11,10},{13,12},{... | collective-permute-start | bytes 24584 | tf_op jit(solution)/shard_map/ppermute | solution.py:17
  9.2 3.8 %copy-start.6 = (s32[1,32]{1,0:T(1,128)S(1)}, s32[1,32]{1,0:T(1,128)}, u32[]{:S(2)}) copy-start(s32[1,32]{1,0:T(1,128)} %param.9) | copy-start | bytes 388
  9.2 4.0 %copy-start.7 = (s32[1,32,128]{2,1,0:T(8,128)S(1)}, s32[1,32,128]{2,1,0:T(8,128)}, u32[]{:S(2)}) copy-start(s32[1,32,128]{2,1,0:T(8,128)} %param.10) | copy-start | bytes 49156
  9.4 8.8 %copy-start.2 = (f32[1,2,32,1024]{3,2,1,0:T(8,128)S(1)}, f32[1,2,32,1024]{3,2,1,0:T(8,128)}, u32[]{:S(2)}) copy-start(f32[1,2,32,1024]{3,2,1,0:T(8,128)} %param.7) | copy-start | bytes 786436
  9.4 8.8 %collective-permute-start.2 = (f32[1,2,32,1024]{3,2,1,0:T(8,128)S(1)}, f32[1,2,32,1024]{3,2,1,0:T(8,128)S(1)}, u32[]{:S(2)}, u32[]{:S(2)}) collective-permute-start(f32[1,2,32,1024]{3,2,1,0:T(8,128)S(1)} %fusion.44), channel_id=1, source_target_pairs={{0,4},{4,8},{8,12},{12,16},{16,20},{20,24},{24,28},{1,5},{5,9},{9,... | collective-permute-start | bytes 786440 | tf_op jit(solution)/shard_map/ppermute | solution.py:25
  13.2 6.3 %copy-start.5 = (f32[1,32,128]{2,1,0:T(8,128)S(1)}, f32[1,32,128]{2,1,0:T(8,128)}, u32[]{:S(2)}) copy-start(f32[1,32,128]{2,1,0:T(8,128)} %param.11) | copy-start | bytes 49156
  18.3 11.0 %collective-permute-start.3 = (f32[1,2,32,1024]{3,2,1,0:T(8,128)S(1)}, f32[1,2,32,1024]{3,2,1,0:T(8,128)S(1)}, u32[]{:S(2)}, u32[]{:S(2)}) collective-permute-start(f32[1,2,32,1024]{3,2,1,0:T(8,128)S(1)} %subtract_multiply_fusion.2), channel_id=1, source_target_pairs={{4,0},{8,4},{12,8},{16,12},{20,16},{24,20},{28,24},{5,1},{9,5},{13... | collective-permute-start | bytes 786440 | tf_op jit(solution)/shard_map/ppermute | solution.py:25
  29.4 4.3 %collective-permute-start.5 = (f32[1,2,1,1024]{3,2,1,0:T(1,128)S(1)}, f32[1,2,1,1024]{3,2,1,0:T(1,128)S(1)}, u32[]{:S(2)}, u32[]{:S(2)}) collective-permute-start(f32[1,2,1,1024]{3,2,1,0:T(1,128)S(1)} %get-tuple-element.45), channel_id=1, source_target_pairs={{0,1},{1,2},{2,3},{4,5},{5,6},{6,7},{8,9},{9,10},{10,11},{12,13},{... | collective-permute-start | bytes 24584 | tf_op jit(solution)/shard_map/ppermute | solution.py:14
  31.6 3.1 %collective-permute-start.4 = (f32[1,2,1,1024]{3,2,1,0:T(1,128)S(1)}, f32[1,2,1,1024]{3,2,1,0:T(1,128)S(1)}, u32[]{:S(2)}, u32[]{:S(2)}) collective-permute-start(f32[1,2,1,1024]{3,2,1,0:T(1,128)S(1)} %get-tuple-element.44), channel_id=1, source_target_pairs={{1,0},{2,1},{3,2},{5,4},{6,5},{7,6},{9,8},{10,9},{11,10},{13,12},{... | collective-permute-start | bytes 24584 | tf_op jit(solution)/shard_map/ppermute | solution.py:17
  79.5 2.7 %collective-permute-start.7 = (f32[1,2,1,1024]{3,2,1,0:T(1,128)S(1)}, f32[1,2,1,1024]{3,2,1,0:T(1,128)S(1)}, u32[]{:S(2)}, u32[]{:S(2)}) collective-permute-start(f32[1,2,1,1024]{3,2,1,0:T(1,128)S(1)} %get-tuple-element.43), channel_id=1, source_target_pairs={{0,1},{1,2},{2,3},{4,5},{5,6},{6,7},{8,9},{9,10},{10,11},{12,13},{... | collective-permute-start | bytes 24584 | tf_op jit(solution)/shard_map/ppermute | solution.py:14
  80.8 5.6 %collective-permute-start.6 = (f32[1,2,1,1024]{3,2,1,0:T(1,128)S(1)}, f32[1,2,1,1024]{3,2,1,0:T(1,128)S(1)}, u32[]{:S(2)}, u32[]{:S(2)}) collective-permute-start(f32[1,2,1,1024]{3,2,1,0:T(1,128)S(1)} %get-tuple-element.42), channel_id=1, source_target_pairs={{1,0},{2,1},{3,2},{5,4},{6,5},{7,6},{9,8},{10,9},{11,10},{13,12},{... | collective-permute-start | bytes 24584 | tf_op jit(solution)/shard_map/ppermute | solution.py:17
  86.6 7.9 %collective-permute-start.8 = (f32[1,2,32,1024]{3,2,1,0:T(8,128)S(1)}, f32[1,2,32,1024]{3,2,1,0:T(8,128)S(1)}, u32[]{:S(2)}, u32[]{:S(2)}) collective-permute-start(f32[1,2,32,1024]{3,2,1,0:T(8,128)S(1)} %fusion.33), channel_id=1, source_target_pairs={{0,4},{4,8},{8,12},{12,16},{16,20},{20,24},{24,28},{1,5},{5,9},{9,... | collective-permute-start | bytes 786440 | tf_op jit(solution)/shard_map/ppermute | solution.py:25
  94.6 11.1 %copy-start.3 = (f32[1,2,32,1024]{3,2,1,0:T(8,128)}, f32[1,2,32,1024]{3,2,1,0:T(8,128)S(1)}, u32[]{:S(2)}) copy-start(f32[1,2,32,1024]{3,2,1,0:T(8,128)S(1)} %subtract_multiply_fusion.1) | copy-start | bytes 786436
  94.6 11.0 %collective-permute-start.9 = (f32[1,2,32,1024]{3,2,1,0:T(8,128)S(1)}, f32[1,2,32,1024]{3,2,1,0:T(8,128)S(1)}, u32[]{:S(2)}, u32[]{:S(2)}) collective-permute-start(f32[1,2,32,1024]{3,2,1,0:T(8,128)S(1)} %subtract_multiply_fusion.1), channel_id=1, source_target_pairs={{4,0},{8,4},{12,8},{16,12},{20,16},{24,20},{28,24},{5,1},{9,5},{13... | collective-permute-start | bytes 786440 | tf_op jit(solution)/shard_map/ppermute | solution.py:25
  105.7 6.0 %collective-permute-start.11 = (f32[1,2,1,1024]{3,2,1,0:T(1,128)S(1)}, f32[1,2,1,1024]{3,2,1,0:T(1,128)S(1)}, u32[]{:S(2)}, u32[]{:S(2)}) collective-permute-start(f32[1,2,1,1024]{3,2,1,0:T(1,128)S(1)} %get-tuple-element.37), channel_id=1, source_target_pairs={{0,1},{1,2},{2,3},{4,5},{5,6},{6,7},{8,9},{9,10},{10,11},{12,13},{... | collective-permute-start | bytes 24584 | tf_op jit(solution)/shard_map/ppermute | solution.py:14
  108.0 3.7 %collective-permute-start.10 = (f32[1,2,1,1024]{3,2,1,0:T(1,128)S(1)}, f32[1,2,1,1024]{3,2,1,0:T(1,128)S(1)}, u32[]{:S(2)}, u32[]{:S(2)}) collective-permute-start(f32[1,2,1,1024]{3,2,1,0:T(1,128)S(1)} %get-tuple-element.36), channel_id=1, source_target_pairs={{1,0},{2,1},{3,2},{5,4},{6,5},{7,6},{9,8},{10,9},{11,10},{13,12},{... | collective-permute-start | bytes 24584 | tf_op jit(solution)/shard_map/ppermute | solution.py:17
  161.0 2.7 %collective-permute-start.13 = (f32[1,2,1,1024]{3,2,1,0:T(1,128)S(1)}, f32[1,2,1,1024]{3,2,1,0:T(1,128)S(1)}, u32[]{:S(2)}, u32[]{:S(2)}) collective-permute-start(f32[1,2,1,1024]{3,2,1,0:T(1,128)S(1)} %get-tuple-element.35), channel_id=1, source_target_pairs={{0,1},{1,2},{2,3},{4,5},{5,6},{6,7},{8,9},{9,10},{10,11},{12,13},{... | collective-permute-start | bytes 24584 | tf_op jit(solution)/shard_map/ppermute | solution.py:14
  162.3 5.6 %collective-permute-start.12 = (f32[1,2,1,1024]{3,2,1,0:T(1,128)S(1)}, f32[1,2,1,1024]{3,2,1,0:T(1,128)S(1)}, u32[]{:S(2)}, u32[]{:S(2)}) collective-permute-start(f32[1,2,1,1024]{3,2,1,0:T(1,128)S(1)} %get-tuple-element.34), channel_id=1, source_target_pairs={{1,0},{2,1},{3,2},{5,4},{6,5},{7,6},{9,8},{10,9},{11,10},{13,12},{... | collective-permute-start | bytes 24584 | tf_op jit(solution)/shard_map/ppermute | solution.py:17
  168.1 7.6 %collective-permute-start.14 = (f32[1,2,32,1024]{3,2,1,0:T(8,128)S(1)}, f32[1,2,32,1024]{3,2,1,0:T(8,128)S(1)}, u32[]{:S(2)}, u32[]{:S(2)}) collective-permute-start(f32[1,2,32,1024]{3,2,1,0:T(8,128)S(1)} %fusion.22), channel_id=1, source_target_pairs={{0,4},{4,8},{8,12},{12,16},{16,20},{20,24},{24,28},{1,5},{5,9},{9,... | collective-permute-start | bytes 786440 | tf_op jit(solution)/shard_map/ppermute | solution.py:25
  175.7 11.1 %copy-start.4 = (f32[1,2,32,1024]{3,2,1,0:T(8,128)}, f32[1,2,32,1024]{3,2,1,0:T(8,128)S(1)}, u32[]{:S(2)}) copy-start(f32[1,2,32,1024]{3,2,1,0:T(8,128)S(1)} %subtract_multiply_fusion) | copy-start | bytes 786436
  175.7 11.0 %collective-permute-start.15 = (f32[1,2,32,1024]{3,2,1,0:T(8,128)S(1)}, f32[1,2,32,1024]{3,2,1,0:T(8,128)S(1)}, u32[]{:S(2)}, u32[]{:S(2)}) collective-permute-start(f32[1,2,32,1024]{3,2,1,0:T(8,128)S(1)} %subtract_multiply_fusion), channel_id=1, source_target_pairs={{4,0},{8,4},{12,8},{16,12},{20,16},{24,20},{28,24},{5,1},{9,5},{13... | collective-permute-start | bytes 786440 | tf_op jit(solution)/shard_map/ppermute | solution.py:25
  186.8 6.7 %collective-permute-start.17 = (f32[1,2,1,1024]{3,2,1,0:T(1,128)S(1)}, f32[1,2,1,1024]{3,2,1,0:T(1,128)S(1)}, u32[]{:S(2)}, u32[]{:S(2)}) collective-permute-start(f32[1,2,1,1024]{3,2,1,0:T(1,128)S(1)} %get-tuple-element.29), channel_id=1, source_target_pairs={{0,1},{1,2},{2,3},{4,5},{5,6},{6,7},{8,9},{9,10},{10,11},{12,13},{... | collective-permute-start | bytes 24584 | tf_op jit(solution)/shard_map/ppermute | solution.py:14
  189.1 4.4 %collective-permute-start.16 = (f32[1,2,1,1024]{3,2,1,0:T(1,128)S(1)}, f32[1,2,1,1024]{3,2,1,0:T(1,128)S(1)}, u32[]{:S(2)}, u32[]{:S(2)}) collective-permute-start(f32[1,2,1,1024]{3,2,1,0:T(1,128)S(1)} %get-tuple-element.28), channel_id=1, source_target_pairs={{1,0},{2,1},{3,2},{5,4},{6,5},{7,6},{9,8},{10,9},{11,10},{13,12},{... | collective-permute-start | bytes 24584 | tf_op jit(solution)/shard_map/ppermute | solution.py:17
where the time goes:
time: 244 us; the launch traced here: 243 us
  blocking collectives  128 us (52%)
  waiting for transfers between devices  45.4 us (19%)
  starting transfers between devices  32.1 us (13%)
  matrix products  13.9 us (6%)
  between operations  11.1 us (5%)
  other arithmetic  6.38 us (3%)
  local copies, waits for them, and re-layouts  6.24 us (3%)
    psum x3, blocking collectives, two_products(): lax.psum((jnp.sum(vector * vector), jnp.sum(vector * image_vec)), ('win',...  128 us
    ppermute x6, waiting for transfers between devices, passed_along(): return lax.ppermute(x, axis, pairs)  33.6 us
    ppermute x6, starting transfers between devices, passed_along(): return lax.ppermute(x, axis, pairs)  12.5 us
    ppermute x6, waiting for transfers between devices, extended(): lax.ppermute(lax.slice_in_dim(block, 0, width, axis=dim), axis, backward)  11.9 us
    ppermute x6, starting transfers between devices, extended(): lax.ppermute(lax.slice_in_dim(block, block.shape[dim] - width, None, axis...  11.8 us
    ppermute x6, starting transfers between devices, extended(): lax.ppermute(lax.slice_in_dim(block, 0, width, axis=dim), axis, backward)  7.75 us
    dot_general x3, matrix products, observe(): jnp.einsum('bjc,bc->bj', cell_hot, picked, precision=lax.Precision.HIGHEST)  5.99 us
  transfers between devices with their start and end apart: 18, of which 10 were waited for; matrix products, arithmetic and copies ran while one was open for 8% of the time, Pallas kernels for 0%

commit v1 on v0

--- a/solution.py
+++ b/solution.py
@@ -82,7 +82,9 @@
         )
 
     def two_products(vector, image_vec):
-        return lax.psum((jnp.sum(vector * vector), jnp.sum(vector * image_vec)), ("win", "tile"))
+        return lax.psum(
+            lax.psum((jnp.sum(vector * vector), jnp.sum(vector * image_vec)), "tile"), "win"
+        )
 
     solution_field = jnp.zeros_like(right_side)
     residual = right_side

time: 244 us -> 199 us (0.82)
  blocking collectives: 128 us -> 86.6 us
    psum x3 -> x6, blocking collectives: 128 us -> 86.6 us  [the longest x3 63.5 us: two_products(): lax.psum(lax.psum((jnp.sum(vector * vector), jnp.sum(vector * image_vec))...]
  transfers between devices with their start and end apart: 18 -> 18, of which waited for: 10 -> 10; matrix products, arithmetic and copies ran while one was open for 8% -> 9% of each run, Pallas kernels for 0% -> 0%
where the time goes in v1:
time: 199 us; the launch traced here: 198 us
  blocking collectives  86.6 us (44%)
  waiting for transfers between devices  43.2 us (22%)
  starting transfers between devices  30.2 us (15%)
  matrix products  13.9 us (7%)
  between operations  11.2 us (6%)
  other arithmetic  6.32 us (3%)
  local copies, waits for them, and re-layouts  6.24 us (3%)
    psum x3, blocking collectives, two_products(): lax.psum(lax.psum((jnp.sum(vector * vector), jnp.sum(vector * image_vec))...  63.5 us
    ppermute x6, waiting for transfers between devices, passed_along(): return lax.ppermute(x, axis, pairs)  32.7 us
    psum x3, blocking collectives, two_products(): lax.psum((jnp.sum(vector * vector), jnp.sum(vector * image_vec)), 'tile')  23.1 us
    ppermute x6, starting transfers between devices, extended(): lax.ppermute(lax.slice_in_dim(block, block.shape[dim] - width, None, axis...  12.3 us
    ppermute x6, waiting for transfers between devices, extended(): lax.ppermute(lax.slice_in_dim(block, 0, width, axis=dim), axis, backward)  10.6 us
    ppermute x6, starting transfers between devices, passed_along(): return lax.ppermute(x, axis, pairs)  10.2 us
    ppermute x6, starting transfers between devices, extended(): lax.ppermute(lax.slice_in_dim(block, 0, width, axis=dim), axis, backward)  7.75 us
    dot_general x3, matrix products, observe(): jnp.einsum('bjc,bc->bj', cell_hot, picked, precision=lax.Precision.HIGHEST)  5.99 us
  transfers between devices with their start and end apart: 18, of which 10 were waited for; matrix products, arithmetic and copies ran while one was open for 9% of the time, Pallas kernels for 0%

profile of v1, /device:TPU:0, one launch (start us, length us, event | category | flops | bytes accessed | tf_op | source)
XLA Modules:
  0.0 197.6 jit_solution(12463373691983276317)
XLA Ops:
  0.7 1.0 fusion.71
  1.6 2.4 %collective-permute-start.1 = (f32[1,2,1,1024]{3,2,1,0:T(1,128)S(1)}, f32[1,2,1,1024]{3,2,1,0:T(1,128)S(1)}, u32[]{:S(2)}, u32[]{:S(2)}) collective-permute-start(f32[1,2,1,1024]{3,2,1,0:T(1,128)S(1)} %get-tuple-element.57), channel_id=1, source_target_pairs={{0,1},{1,2},{2,3},{4,5},{5,6},{6,7},{8,9},{9,10},{10,11},{12,13},{... | collective-permute-start | bytes 24584 | tf_op jit(solution)/shard_map/ppermute | solution.py:14
  4.0 1.3 collective-permute-start
  5.3 1.2 fusion.70
  6.5 0.1 fusion.69
  6.7 2.5 %collective-permute-done = f32[1,2,1,1024]{3,2,1,0:T(1,128)S(1)} collective-permute-done((f32[1,2,1,1024]{3,2,1,0:T(1,128)S(1)}, f32[1,2,1,1024]{3,2,1,0:T(1,128)S(1)}, u32[]{:S(2)}, u32[]{:S(2)}) %collective-permute-start) | collective-permute-done | bytes 8224 | tf_op jit(solution)/shard_map/ppermute | solution.py:17
  9.2 0.2 fusion.44
  9.4 3.6 %collective-permute-start.2 = (f32[1,2,32,1024]{3,2,1,0:T(8,128)S(1)}, f32[1,2,32,1024]{3,2,1,0:T(8,128)S(1)}, u32[]{:S(2)}, u32[]{:S(2)}) collective-permute-start(f32[1,2,32,1024]{3,2,1,0:T(8,128)S(1)} %fusion.44), channel_id=1, source_target_pairs={{0,4},{4,8},{8,12},{12,16},{16,20},{20,24},{24,28},{1,5},{5,9},{9,... | collective-permute-start | bytes 786440 | tf_op jit(solution)/shard_map/ppermute | solution.py:25
  13.0 0.2 fusion.50
  13.3 2.0 %fusion.5 = f32[32,1,128]{2,1,0:T(1,128)S(1)} fusion(f32[32,128,1]{1,2,0:T(1,128)S(1)} %bitcast.115, s32[32,128]{1,0:T(8,128)S(1)} %bitcast.121), kind=kOutput, calls=%fused_computation.6 | convolution fusion | flops 6815744 | bytes 49152 | tf_op jit(solution)/shard_map/bjc,bc->bj/dot_general | solution.py:56
  15.3 3.0 %collective-permute-done.2 = f32[1,2,32,1024]{3,2,1,0:T(8,128)S(1)} collective-permute-done((f32[1,2,32,1024]{3,2,1,0:T(8,128)S(1)}, f32[1,2,32,1024]{3,2,1,0:T(8,128)S(1)}, u32[]{:S(2)}, u32[]{:S(2)}) %collective-permute-start.2) | collective-permute-done | bytes 262176 | tf_op jit(solution)/shard_map/ppermute | solution.py:25
  18.3 1.3 collective-permute-start.3
  19.6 1.5 fusion.4
  21.1 8.2 %collective-permute-done.3 = f32[1,2,32,1024]{3,2,1,0:T(8,128)S(1)} collective-permute-done((f32[1,2,32,1024]{3,2,1,0:T(8,128)S(1)}, f32[1,2,32,1024]{3,2,1,0:T(8,128)S(1)}, u32[]{:S(2)}, u32[]{:S(2)}) %collective-permute-start.3) | collective-permute-done | bytes 262176 | tf_op jit(solution)/shard_map/ppermute | solution.py:25
  29.4 2.3 %collective-permute-start.5 = (f32[1,2,1,1024]{3,2,1,0:T(1,128)S(1)}, f32[1,2,1,1024]{3,2,1,0:T(1,128)S(1)}, u32[]{:S(2)}, u32[]{:S(2)}) collective-permute-start(f32[1,2,1,1024]{3,2,1,0:T(1,128)S(1)} %get-tuple-element.51), channel_id=1, source_target_pairs={{0,1},{1,2},{2,3},{4,5},{5,6},{6,7},{8,9},{9,10},{10,11},{12,13},{... | collective-permute-start | bytes 24584 | tf_op jit(solution)/shard_map/ppermute | solution.py:14
  31.6 1.3 collective-permute-start.4
  32.9 0.5 fusion.49
  33.5 0.1 slice.248
  33.7 1.0 collective-permute-done.4
  34.7 0.8 multiply_reduce_fusion.4
  35.5 8.2 %all-reduce.5 = (f32[]{:T(128)}, f32[]{:T(128)}) all-reduce(f32[]{:T(128)} %get-tuple-element.7, f32[]{:T(128)} %get-tuple-element.6), channel_id=1, replica_groups=mesh['win'=8,'tile'=4] {'tile'}, use_global_device_ids=true, to_apply=%region_1.2 | all-reduce | flops 2 | bytes 16 | tf_op jit(solution)/shard_map/psum | solution.py:86
  43.7 22.1 %all-reduce.2 = (f32[]{:T(128)}, f32[]{:T(128)}) all-reduce(f32[]{:T(128)} %get-tuple-element.18, f32[]{:T(128)} %get-tuple-element.19), channel_id=1, replica_groups=mesh['win'=8,'tile'=4] {'win'}, use_global_device_ids=true, to_apply=%region_2.3 | all-reduce | flops 2 | bytes 16 | tf_op jit(solution)/shard_map/psum | solution.py:85
  67.1 0.1 fusion.66
  67.3 1.3 collective-permute-start.7
  68.6 1.3 collective-permute-start.6
  70.0 3.5 %collective-permute-done.6 = f32[1,2,1,1024]{3,2,1,0:T(1,128)S(1)} collective-permute-done((f32[1,2,1,1024]{3,2,1,0:T(1,128)S(1)}, f32[1,2,1,1024]{3,2,1,0:T(1,128)S(1)}, u32[]{:S(2)}, u32[]{:S(2)}) %collective-permute-start.6) | collective-permute-done | bytes 8224 | tf_op jit(solution)/shard_map/ppermute | solution.py:17
  73.5 0.2 fusion.33
  73.7 1.4 collective-permute-start.8
  75.1 0.2 fusion.48
  75.4 2.0 %fusion.3 = f32[32,1,128]{2,1,0:T(1,128)S(1)} fusion(f32[32,128,1]{1,2,0:T(1,128)S(1)} %bitcast.117, s32[32,128]{1,0:T(8,128)S(1)} %bitcast.123), kind=kOutput, calls=%fused_computation.4 | convolution fusion | flops 6815744 | bytes 49152 | tf_op jit(solution)/shard_map/bjc,bc->bj/dot_general | solution.py:56
  77.4 2.8 %collective-permute-done.8 = f32[1,2,32,1024]{3,2,1,0:T(8,128)S(1)} collective-permute-done((f32[1,2,32,1024]{3,2,1,0:T(8,128)S(1)}, f32[1,2,32,1024]{3,2,1,0:T(8,128)S(1)}, u32[]{:S(2)}, u32[]{:S(2)}) %collective-permute-start.8) | collective-permute-done | bytes 262176 | tf_op jit(solution)/shard_map/ppermute | solution.py:25
  80.2 1.3 collective-permute-start.9
  81.6 1.5 fusion.2
  83.0 8.0 %collective-permute-done.9 = f32[1,2,32,1024]{3,2,1,0:T(8,128)S(1)} collective-permute-done((f32[1,2,32,1024]{3,2,1,0:T(8,128)S(1)}, f32[1,2,32,1024]{3,2,1,0:T(8,128)S(1)}, u32[]{:S(2)}, u32[]{:S(2)}) %collective-permute-start.9) | collective-permute-done | bytes 262176 | tf_op jit(solution)/shard_map/ppermute | solution.py:25
  91.2 2.5 %collective-permute-start.11 = (f32[1,2,1,1024]{3,2,1,0:T(1,128)S(1)}, f32[1,2,1,1024]{3,2,1,0:T(1,128)S(1)}, u32[]{:S(2)}, u32[]{:S(2)}) collective-permute-start(f32[1,2,1,1024]{3,2,1,0:T(1,128)S(1)} %get-tuple-element.43), channel_id=1, source_target_pairs={{0,1},{1,2},{2,3},{4,5},{5,6},{6,7},{8,9},{9,10},{10,11},{12,13},{... | collective-permute-start | bytes 24584 | tf_op jit(solution)/shard_map/ppermute | solution.py:14
  93.6 1.3 collective-permute-start.10
  94.9 1.2 fusion.47
  96.1 1.0 reshape.243
  97.1 0.1 slice.260
  97.3 1.8 multiply_reduce_fusion.2
  99.1 7.5 %all-reduce.4 = (f32[]{:T(128)}, f32[]{:T(128)}) all-reduce(f32[]{:T(128)} %get-tuple-element.5, f32[]{:T(128)} %get-tuple-element.4), channel_id=1, replica_groups=mesh['win'=8,'tile'=4] {'tile'}, use_global_device_ids=true, to_apply=%region_7.8 | all-reduce | flops 2 | bytes 16 | tf_op jit(solution)/shard_map/psum | solution.py:86
  106.6 20.7 %all-reduce.1 = (f32[]{:T(128)}, f32[]{:T(128)}) all-reduce(f32[]{:T(128)} %get-tuple-element.16, f32[]{:T(128)} %get-tuple-element.17), channel_id=1, replica_groups=mesh['win'=8,'tile'=4] {'win'}, use_global_device_ids=true, to_apply=%region_8.9 | all-reduce | flops 2 | bytes 16 | tf_op jit(solution)/shard_map/psum | solution.py:85
  132.1 0.1 fusion.62
  132.3 1.3 collective-permute-start.13
  133.6 1.3 collective-permute-start.12
  134.9 0.1 fusion.61
  135.0 3.5 %collective-permute-done.12 = f32[1,2,1,1024]{3,2,1,0:T(1,128)S(1)} collective-permute-done((f32[1,2,1,1024]{3,2,1,0:T(1,128)S(1)}, f32[1,2,1,1024]{3,2,1,0:T(1,128)S(1)}, u32[]{:S(2)}, u32[]{:S(2)}) %collective-permute-start.12) | collective-permute-done | bytes 8224 | tf_op jit(solution)/shard_map/ppermute | solution.py:17
  138.5 0.2 fusion.22
  138.7 1.3 collective-permute-start.14
  140.0 0.2 fusion.46
  140.2 2.0 %fusion.1 = f32[32,1,128]{2,1,0:T(1,128)S(1)} fusion(f32[32,128,1]{1,2,0:T(1,128)S(1)} %bitcast.119, s32[32,128]{1,0:T(8,128)S(1)} %bitcast.125), kind=kOutput, calls=%fused_computation.2 | convolution fusion | flops 6815744 | bytes 49152 | tf_op jit(solution)/shard_map/bjc,bc->bj/dot_general | solution.py:56
  142.2 2.7 %collective-permute-done.14 = f32[1,2,32,1024]{3,2,1,0:T(8,128)S(1)} collective-permute-done((f32[1,2,32,1024]{3,2,1,0:T(8,128)S(1)}, f32[1,2,32,1024]{3,2,1,0:T(8,128)S(1)}, u32[]{:S(2)}, u32[]{:S(2)}) %collective-permute-start.14) | collective-permute-done | bytes 262176 | tf_op jit(solution)/shard_map/ppermute | solution.py:25
  145.0 1.3 collective-permute-start.15
  146.3 1.5 fusion
  147.8 7.9 %collective-permute-done.15 = f32[1,2,32,1024]{3,2,1,0:T(8,128)S(1)} collective-permute-done((f32[1,2,32,1024]{3,2,1,0:T(8,128)S(1)}, f32[1,2,32,1024]{3,2,1,0:T(8,128)S(1)}, u32[]{:S(2)}, u32[]{:S(2)}) %collective-permute-start.15) | collective-permute-done | bytes 262176 | tf_op jit(solution)/shard_map/ppermute | solution.py:25
  155.8 2.6 %collective-permute-start.17 = (f32[1,2,1,1024]{3,2,1,0:T(1,128)S(1)}, f32[1,2,1,1024]{3,2,1,0:T(1,128)S(1)}, u32[]{:S(2)}, u32[]{:S(2)}) collective-permute-start(f32[1,2,1,1024]{3,2,1,0:T(1,128)S(1)} %get-tuple-element.35), channel_id=1, source_target_pairs={{0,1},{1,2},{2,3},{4,5},{5,6},{6,7},{8,9},{9,10},{10,11},{12,13},{... | collective-permute-start | bytes 24584 | tf_op jit(solution)/shard_map/ppermute | solution.py:14
  158.4 1.3 collective-permute-start.16
  159.7 1.2 fusion.45
  160.8 1.7 reshape.245
  162.5 0.1 slice.272
  162.8 1.8 multiply_reduce_fusion
  164.6 7.4 %all-reduce.3 = (f32[]{:T(128)}, f32[]{:T(128)}) all-reduce(f32[]{:T(128)} %get-tuple-element.3, f32[]{:T(128)} %get-tuple-element.2), channel_id=1, replica_groups=mesh['win'=8,'tile'=4] {'tile'}, use_global_device_ids=true, to_apply=%region_13.14 | all-reduce | flops 2 | bytes 16 | tf_op jit(solution)/shard_map/psum | solution.py:86
  172.0 20.7 %all-reduce = (f32[]{:T(128)}, f32[]{:T(128)}) all-reduce(f32[]{:T(128)} %get-tuple-element.14, f32[]{:T(128)} %get-tuple-element.15), channel_id=1, replica_groups=mesh['win'=8,'tile'=4] {'win'}, use_global_device_ids=true, to_apply=%region_14.15 | all-reduce | flops 2 | bytes 16 | tf_op jit(solution)/shard_map/psum | solution.py:85
  196.7 0.9 multiply_subtract_fusion
  (51 shorter events, 1.1 us)
Async XLA Ops:
  0.6 5.9 %copy-start.1 = (f32[1,2,32,1024]{3,2,1,0:T(8,128)S(1)}, f32[1,2,32,1024]{3,2,1,0:T(8,128)}, u32[]{:S(2)}) copy-start(f32[1,2,32,1024]{3,2,1,0:T(8,128)} %param.6) | copy-start | bytes 786436
  0.6 8.6 %copy-start = (f32[4,1,2,32,1024]{4,3,2,1,0:T(8,128)S(1)}, f32[4,1,2,32,1024]{4,3,2,1,0:T(8,128)}, u32[]{:S(2)}) copy-start(f32[4,1,2,32,1024]{4,3,2,1,0:T(8,128)} %param.8) | copy-start | bytes 3145732
  1.6 5.0 %collective-permute-start.1 = (f32[1,2,1,1024]{3,2,1,0:T(1,128)S(1)}, f32[1,2,1,1024]{3,2,1,0:T(1,128)S(1)}, u32[]{:S(2)}, u32[]{:S(2)}) collective-permute-start(f32[1,2,1,1024]{3,2,1,0:T(1,128)S(1)} %get-tuple-element.57), channel_id=1, source_target_pairs={{0,1},{1,2},{2,3},{4,5},{5,6},{6,7},{8,9},{9,10},{10,11},{12,13},{... | collective-permute-start | bytes 24584 | tf_op jit(solution)/shard_map/ppermute | solution.py:14
  4.0 5.2 %collective-permute-start = (f32[1,2,1,1024]{3,2,1,0:T(1,128)S(1)}, f32[1,2,1,1024]{3,2,1,0:T(1,128)S(1)}, u32[]{:S(2)}, u32[]{:S(2)}) collective-permute-start(f32[1,2,1,1024]{3,2,1,0:T(1,128)S(1)} %get-tuple-element.56), channel_id=1, source_target_pairs={{1,0},{2,1},{3,2},{5,4},{6,5},{7,6},{9,8},{10,9},{11,10},{13,12},{... | collective-permute-start | bytes 24584 | tf_op jit(solution)/shard_map/ppermute | solution.py:17
  9.2 3.8 %copy-start.6 = (s32[1,32]{1,0:T(1,128)S(1)}, s32[1,32]{1,0:T(1,128)}, u32[]{:S(2)}) copy-start(s32[1,32]{1,0:T(1,128)} %param.9) | copy-start | bytes 388
  9.2 4.0 %copy-start.7 = (s32[1,32,128]{2,1,0:T(8,128)S(1)}, s32[1,32,128]{2,1,0:T(8,128)}, u32[]{:S(2)}) copy-start(s32[1,32,128]{2,1,0:T(8,128)} %param.10) | copy-start | bytes 49156
  9.4 8.8 %copy-start.2 = (f32[1,2,32,1024]{3,2,1,0:T(8,128)S(1)}, f32[1,2,32,1024]{3,2,1,0:T(8,128)}, u32[]{:S(2)}) copy-start(f32[1,2,32,1024]{3,2,1,0:T(8,128)} %param.7) | copy-start | bytes 786436
  9.4 8.8 %collective-permute-start.2 = (f32[1,2,32,1024]{3,2,1,0:T(8,128)S(1)}, f32[1,2,32,1024]{3,2,1,0:T(8,128)S(1)}, u32[]{:S(2)}, u32[]{:S(2)}) collective-permute-start(f32[1,2,32,1024]{3,2,1,0:T(8,128)S(1)} %fusion.44), channel_id=1, source_target_pairs={{0,4},{4,8},{8,12},{12,16},{16,20},{20,24},{24,28},{1,5},{5,9},{9,... | collective-permute-start | bytes 786440 | tf_op jit(solution)/shard_map/ppermute | solution.py:25
  13.2 6.3 %copy-start.5 = (f32[1,32,128]{2,1,0:T(8,128)S(1)}, f32[1,32,128]{2,1,0:T(8,128)}, u32[]{:S(2)}) copy-start(f32[1,32,128]{2,1,0:T(8,128)} %param.11) | copy-start | bytes 49156
  18.3 11.0 %collective-permute-start.3 = (f32[1,2,32,1024]{3,2,1,0:T(8,128)S(1)}, f32[1,2,32,1024]{3,2,1,0:T(8,128)S(1)}, u32[]{:S(2)}, u32[]{:S(2)}) collective-permute-start(f32[1,2,32,1024]{3,2,1,0:T(8,128)S(1)} %subtract_multiply_fusion.2), channel_id=1, source_target_pairs={{4,0},{8,4},{12,8},{16,12},{20,16},{24,20},{28,24},{5,1},{9,5},{13... | collective-permute-start | bytes 786440 | tf_op jit(solution)/shard_map/ppermute | solution.py:25
  29.4 4.3 %collective-permute-start.5 = (f32[1,2,1,1024]{3,2,1,0:T(1,128)S(1)}, f32[1,2,1,1024]{3,2,1,0:T(1,128)S(1)}, u32[]{:S(2)}, u32[]{:S(2)}) collective-permute-start(f32[1,2,1,1024]{3,2,1,0:T(1,128)S(1)} %get-tuple-element.51), channel_id=1, source_target_pairs={{0,1},{1,2},{2,3},{4,5},{5,6},{6,7},{8,9},{9,10},{10,11},{12,13},{... | collective-permute-start | bytes 24584 | tf_op jit(solution)/shard_map/ppermute | solution.py:14
  31.6 3.1 %collective-permute-start.4 = (f32[1,2,1,1024]{3,2,1,0:T(1,128)S(1)}, f32[1,2,1,1024]{3,2,1,0:T(1,128)S(1)}, u32[]{:S(2)}, u32[]{:S(2)}) collective-permute-start(f32[1,2,1,1024]{3,2,1,0:T(1,128)S(1)} %get-tuple-element.50), channel_id=1, source_target_pairs={{1,0},{2,1},{3,2},{5,4},{6,5},{7,6},{9,8},{10,9},{11,10},{13,12},{... | collective-permute-start | bytes 24584 | tf_op jit(solution)/shard_map/ppermute | solution.py:17
  67.3 2.7 %collective-permute-start.7 = (f32[1,2,1,1024]{3,2,1,0:T(1,128)S(1)}, f32[1,2,1,1024]{3,2,1,0:T(1,128)S(1)}, u32[]{:S(2)}, u32[]{:S(2)}) collective-permute-start(f32[1,2,1,1024]{3,2,1,0:T(1,128)S(1)} %get-tuple-element.49), channel_id=1, source_target_pairs={{0,1},{1,2},{2,3},{4,5},{5,6},{6,7},{8,9},{9,10},{10,11},{12,13},{... | collective-permute-start | bytes 24584 | tf_op jit(solution)/shard_map/ppermute | solution.py:14
  68.6 4.9 %collective-permute-start.6 = (f32[1,2,1,1024]{3,2,1,0:T(1,128)S(1)}, f32[1,2,1,1024]{3,2,1,0:T(1,128)S(1)}, u32[]{:S(2)}, u32[]{:S(2)}) collective-permute-start(f32[1,2,1,1024]{3,2,1,0:T(1,128)S(1)} %get-tuple-element.48), channel_id=1, source_target_pairs={{1,0},{2,1},{3,2},{5,4},{6,5},{7,6},{9,8},{10,9},{11,10},{13,12},{... | collective-permute-start | bytes 24584 | tf_op jit(solution)/shard_map/ppermute | solution.py:17
  73.7 6.5 %collective-permute-start.8 = (f32[1,2,32,1024]{3,2,1,0:T(8,128)S(1)}, f32[1,2,32,1024]{3,2,1,0:T(8,128)S(1)}, u32[]{:S(2)}, u32[]{:S(2)}) collective-permute-start(f32[1,2,32,1024]{3,2,1,0:T(8,128)S(1)} %fusion.33), channel_id=1, source_target_pairs={{0,4},{4,8},{8,12},{12,16},{16,20},{20,24},{24,28},{1,5},{5,9},{9,... | collective-permute-start | bytes 786440 | tf_op jit(solution)/shard_map/ppermute | solution.py:25
  80.2 10.9 %copy-start.3 = (f32[1,2,32,1024]{3,2,1,0:T(8,128)}, f32[1,2,32,1024]{3,2,1,0:T(8,128)S(1)}, u32[]{:S(2)}) copy-start(f32[1,2,32,1024]{3,2,1,0:T(8,128)S(1)} %subtract_multiply_fusion.1) | copy-start | bytes 786436
  80.2 10.8 %collective-permute-start.9 = (f32[1,2,32,1024]{3,2,1,0:T(8,128)S(1)}, f32[1,2,32,1024]{3,2,1,0:T(8,128)S(1)}, u32[]{:S(2)}, u32[]{:S(2)}) collective-permute-start(f32[1,2,32,1024]{3,2,1,0:T(8,128)S(1)} %subtract_multiply_fusion.1), channel_id=1, source_target_pairs={{4,0},{8,4},{12,8},{16,12},{20,16},{24,20},{28,24},{5,1},{9,5},{13... | collective-permute-start | bytes 786440 | tf_op jit(solution)/shard_map/ppermute | solution.py:25
  91.2 6.2 %collective-permute-start.11 = (f32[1,2,1,1024]{3,2,1,0:T(1,128)S(1)}, f32[1,2,1,1024]{3,2,1,0:T(1,128)S(1)}, u32[]{:S(2)}, u32[]{:S(2)}) collective-permute-start(f32[1,2,1,1024]{3,2,1,0:T(1,128)S(1)} %get-tuple-element.43), channel_id=1, source_target_pairs={{0,1},{1,2},{2,3},{4,5},{5,6},{6,7},{8,9},{9,10},{10,11},{12,13},{... | collective-permute-start | bytes 24584 | tf_op jit(solution)/shard_map/ppermute | solution.py:14
  93.6 3.7 %collective-permute-start.10 = (f32[1,2,1,1024]{3,2,1,0:T(1,128)S(1)}, f32[1,2,1,1024]{3,2,1,0:T(1,128)S(1)}, u32[]{:S(2)}, u32[]{:S(2)}) collective-permute-start(f32[1,2,1,1024]{3,2,1,0:T(1,128)S(1)} %get-tuple-element.42), channel_id=1, source_target_pairs={{1,0},{2,1},{3,2},{5,4},{6,5},{7,6},{9,8},{10,9},{11,10},{13,12},{... | collective-permute-start | bytes 24584 | tf_op jit(solution)/shard_map/ppermute | solution.py:17
  132.3 2.7 %collective-permute-start.13 = (f32[1,2,1,1024]{3,2,1,0:T(1,128)S(1)}, f32[1,2,1,1024]{3,2,1,0:T(1,128)S(1)}, u32[]{:S(2)}, u32[]{:S(2)}) collective-permute-start(f32[1,2,1,1024]{3,2,1,0:T(1,128)S(1)} %get-tuple-element.41), channel_id=1, source_target_pairs={{0,1},{1,2},{2,3},{4,5},{5,6},{6,7},{8,9},{9,10},{10,11},{12,13},{... | collective-permute-start | bytes 24584 | tf_op jit(solution)/shard_map/ppermute | solution.py:14
  133.6 4.9 %collective-permute-start.12 = (f32[1,2,1,1024]{3,2,1,0:T(1,128)S(1)}, f32[1,2,1,1024]{3,2,1,0:T(1,128)S(1)}, u32[]{:S(2)}, u32[]{:S(2)}) collective-permute-start(f32[1,2,1,1024]{3,2,1,0:T(1,128)S(1)} %get-tuple-element.40), channel_id=1, source_target_pairs={{1,0},{2,1},{3,2},{5,4},{6,5},{7,6},{9,8},{10,9},{11,10},{13,12},{... | collective-permute-start | bytes 24584 | tf_op jit(solution)/shard_map/ppermute | solution.py:17
  138.7 6.3 %collective-permute-start.14 = (f32[1,2,32,1024]{3,2,1,0:T(8,128)S(1)}, f32[1,2,32,1024]{3,2,1,0:T(8,128)S(1)}, u32[]{:S(2)}, u32[]{:S(2)}) collective-permute-start(f32[1,2,32,1024]{3,2,1,0:T(8,128)S(1)} %fusion.22), channel_id=1, source_target_pairs={{0,4},{4,8},{8,12},{12,16},{16,20},{20,24},{24,28},{1,5},{5,9},{9,... | collective-permute-start | bytes 786440 | tf_op jit(solution)/shard_map/ppermute | solution.py:25
  145.0 10.8 %copy-start.4 = (f32[1,2,32,1024]{3,2,1,0:T(8,128)}, f32[1,2,32,1024]{3,2,1,0:T(8,128)S(1)}, u32[]{:S(2)}) copy-start(f32[1,2,32,1024]{3,2,1,0:T(8,128)S(1)} %subtract_multiply_fusion) | copy-start | bytes 786436
  145.0 10.7 %collective-permute-start.15 = (f32[1,2,32,1024]{3,2,1,0:T(8,128)S(1)}, f32[1,2,32,1024]{3,2,1,0:T(8,128)S(1)}, u32[]{:S(2)}, u32[]{:S(2)}) collective-permute-start(f32[1,2,32,1024]{3,2,1,0:T(8,128)S(1)} %subtract_multiply_fusion), channel_id=1, source_target_pairs={{4,0},{8,4},{12,8},{16,12},{20,16},{24,20},{28,24},{5,1},{9,5},{13... | collective-permute-start | bytes 786440 | tf_op jit(solution)/shard_map/ppermute | solution.py:25
  155.8 7.0 %collective-permute-start.17 = (f32[1,2,1,1024]{3,2,1,0:T(1,128)S(1)}, f32[1,2,1,1024]{3,2,1,0:T(1,128)S(1)}, u32[]{:S(2)}, u32[]{:S(2)}) collective-permute-start(f32[1,2,1,1024]{3,2,1,0:T(1,128)S(1)} %get-tuple-element.35), channel_id=1, source_target_pairs={{0,1},{1,2},{2,3},{4,5},{5,6},{6,7},{8,9},{9,10},{10,11},{12,13},{... | collective-permute-start | bytes 24584 | tf_op jit(solution)/shard_map/ppermute | solution.py:14
  158.4 4.4 %collective-permute-start.16 = (f32[1,2,1,1024]{3,2,1,0:T(1,128)S(1)}, f32[1,2,1,1024]{3,2,1,0:T(1,128)S(1)}, u32[]{:S(2)}, u32[]{:S(2)}) collective-permute-start(f32[1,2,1,1024]{3,2,1,0:T(1,128)S(1)} %get-tuple-element.34), channel_id=1, source_target_pairs={{1,0},{2,1},{3,2},{5,4},{6,5},{7,6},{9,8},{10,9},{11,10},{13,12},{... | collective-permute-start | bytes 24584 | tf_op jit(solution)/shard_map/ppermute | solution.py:17
